TPU v7x, 32 devices: a whole 2x2x4 slice. The times are simulated.
32 devices in a mesh: lev: 4 (over x, core), lon: 8 (over z, y).
Axes of the slice: x: 2, y: 2, z: 4, core: 2. Of those that a mesh axis runs over, the one named last changes fastest.
Arguments:
- previous: float32 [36, 64, 4096], P('lev', None, 'lon'), may hold values from -4 to 4
- loss_matrix: float32 [36, 64, 64], P('lev'), may hold values from -3 to 10, as said below
- pair_matrix: float32 [36, 64, 64], P('lev'), may hold values from -0.1875 to 0.1875
- diffusivity: float32 [36], P('lev'), may hold values from 200 to 2000
- mixing: float32 [36], P('lev'), may hold values from 0.1 to 1
Outputs:
- concentration: float32 [36, 64, 4096], P('lev', None, 'lon')
- level_variance: float32 [36, 64], P('lev')
Inputs may be any that keep to these rules, and one draw needn't show every extreme that they name: `loss_matrix`: each of the 36 blocks is symmetric and at least 0.05 times the identity in the positive definite order.
All inputs are finite; a program needn't handle non-finite values.
Results may differ from a plain program's by a relative error of at most 0.00045.
Values sent between devices are 32-bit elements; how exact they have to be, the bound alone decides.
A program may use at most 64 MiB of HBM per device.

v0:
```python
import functools

import jax
import jax.numpy as jnp
from jax import lax
from jax.experimental import pallas as pl
from jax.experimental.pallas import tpu as pltpu
from jax.sharding import PartitionSpec as P

LEAST = 1.05
MOST = 10.0
HIGHEST = lax.Precision.HIGHEST
SMEM = pl.BlockSpec(memory_space=pltpu.SMEM)
VMEM = pl.BlockSpec(memory_space=pltpu.VMEM)


def dot(a, b, dims=((1,), (0,))):
    return lax.dot_general(
        a, b, (dims, ((), ())), precision=HIGHEST, preferred_element_type=jnp.float32
    )


def dot_t(a, b):
    return dot(a, b, ((1,), (1,)))


def eye_of(size):
    rows = lax.broadcasted_iota(jnp.int32, (size, size), 0)
    cols = lax.broadcasted_iota(jnp.int32, (size, size), 1)
    return rows == cols


def invert_all(blocks, floors, steps):
    size = blocks[0].shape[0]
    unit = jnp.where(eye_of(size), 1.0, 0.0).astype(jnp.float32)
    start, worst = [], None
    for a, lo in zip(blocks, floors):
        hi = jnp.max(jnp.sum(jnp.abs(a), axis=0, keepdims=True), axis=1, keepdims=True)
        hi = jnp.clip(hi, lo, lo * spread(size))
        scale = 2.0 / (hi + lo)
        rho = (hi - lo) / (hi + lo)
        start.append((scale, a))
        worst = rho if worst is None else jnp.maximum(worst, rho)

    def grow(rho):
        square = rho * rho
        return square / (2.0 - square), 2.0 / (2.0 - square)

    rho, gain = grow(worst)
    start = [(gain * scale) * (2.0 * unit - scale * a) for scale, a in start]

    def step(carry):
        rho, *xs = carry
        rest = [unit - dot(a, x) for a, x in zip(blocks, xs)]
        rho, gain = grow(rho)
        return (rho, *[gain * (x + dot(x, r)) for x, r in zip(xs, rest)])

    if steps is None:
        return lax.while_loop(lambda carry: jnp.max(carry[0]) > 3e-8, step, (rho, *start))[1:]
    return lax.fori_loop(0, steps, lambda i, carry: step(carry), (rho, *start))[1:]


def spread(size):
    return (1.0 + MOST * size) / (0.96 * LEAST)


def enough_steps(condition):
    rho, steps = (condition - 1.0) / (condition + 1.0), -1
    while rho > 3e-8:
        rho, steps = rho * rho / (2.0 - rho * rho), steps + 1
    return steps


def plan(lo, hi, out):
    if lo >= hi:
        return 0
    mid = lo + (hi - lo) // 2
    depth = 1 + max(plan(lo, mid, out), plan(mid + 1, hi, out))
    out.setdefault(depth, []).append((lo, mid, hi))
    return depth


def dense_inverse(diag, low, floor_diag, floor_low, steps=None):
    count, size = len(diag), diag[0].shape[0]
    unit = jnp.where(eye_of(size), 1.0, 0.0).astype(jnp.float32)
    by_depth, done, thin = {}, {}, {}
    plan(0, count, by_depth)
    for depth in sorted(by_depth):
        nodes = by_depth[depth]
        schur, arms, floors, thin_arms = [], [], [], []
        for lo, mid, hi in nodes:
            s, parts = diag[mid], []
            t, thin_parts = floor_diag[mid], []
            if lo < mid:
                arm = low_right(done[lo, mid][-1], low, mid, False)
                s = s - low(mid, arm[-size:])
                parts.append(arm)
                thin_parts += [floor_low[mid] * x for x in thin[lo, mid][-1]]
                t = t - floor_low[mid] * thin_parts[-1]
            parts.append(unit)
            thin_parts.append(1.0)
            if mid + 1 < hi:
                arm = low_right(done[mid + 1, hi][0], low, mid + 1, True)
                s = s - low(mid + 1, arm[:size], True)
                parts.append(arm)
                thin_arm = [floor_low[mid + 1] * x for x in thin[mid + 1, hi][0]]
                t = t - floor_low[mid + 1] * thin_arm[0]
                thin_parts += thin_arm
            schur.append(s)
            floors.append(t)
            arms.append(jnp.concatenate(parts, axis=0) if len(parts) > 1 else parts[0])
            thin_arms.append(thin_parts)
        inverses = invert_all(schur, [0.97 * t for t in floors], steps)
        for (lo, mid, hi), v, z, thin_v, t in zip(nodes, arms, inverses, thin_arms, floors):
            thin[lo, hi] = [[a * b / t for b in thin_v] for a in thin_v]
            for a, b in ((lo, mid), (mid + 1, hi)):
                for i in range(a, b):
                    for j in range(a, b):
                        thin[lo, hi][i - lo][j - lo] += thin[a, b][i - a][j - a]
            if hi - lo == 1:
                done[lo, hi] = [z]
                continue
            w = dot(v, z)
            panels = []
            for k in range(lo, hi):
                vk = v[(k - lo) * size : (k - lo + 1) * size]
                new = w if k == mid else dot_t(w, vk)
                pieces = []
                for a, b in ((lo, mid), (mid, mid + 1), (mid + 1, hi)):
                    if a >= b:
                        continue
                    piece = new[(a - lo) * size : (b - lo) * size]
                    if a <= k < b and k != mid:
                        piece = piece + done[a, b][k - a]
                    pieces.append(piece)
                panels.append(jnp.concatenate(pieces, axis=0) if len(pieces) > 1 else pieces[0])
            done[lo, hi] = panels
    return done[0, count], thin[0, count]


def low_right(panel, low, k, plain):
    return low(k, panel, not plain, True)


def split(x):
    high = x.astype(jnp.bfloat16)
    return high, (x - high.astype(jnp.float32)).astype(jnp.bfloat16)


def dot3(a_high, a_low, b):
    b_high, b_low = split(b)
    mul = functools.partial(jnp.dot, preferred_element_type=jnp.float32)
    return mul(a_high, b_high) + (mul(a_low, b_high) + mul(a_high, b_low))


def factor_kernel(links_ref, top_ref, loss_ref, high_ref, low_ref, ends_ref, send_ref):
    levels, size = loss_ref.shape[0], loss_ref.shape[1]
    inner = levels - 1
    on_diag = eye_of(size)
    top_link, inner_link = top_ref[0:1, 0:1], jnp.full((1, 1), links_ref[inner - 1])
    links = [jnp.full((1, 1), links_ref[k]) for k in range(levels)]

    def diag_of(k):
        above = top_link if k == 0 else links[k - 1]
        return loss_ref[k] + jnp.where(on_diag, 1.0 + above + links[k], 0.0)

    def low(k, x, transposed=False, right=False):
        return links_ref[k - 1] * x

    floor_diag = [
        LEAST + links[k] + (top_link if k == 0 else links[k - 1]) for k in range(levels)
    ]
    panels, thin = dense_inverse(
        [diag_of(k) for k in range(inner)], low, floor_diag[:inner], [top_link] + links[: inner - 1]
    )
    for k, panel in enumerate(panels):
        high, rest = split(panel)
        high_ref[:, k * size : (k + 1) * size] = high
        low_ref[:, k * size : (k + 1) * size] = rest
    ends_ref[0] = top_link * panels[0]
    ends_ref[1] = inner_link * panels[-1]
    blocks = [
        (
            diag_of(inner) - inner_link * inner_link * panels[-1][-size:],
            floor_diag[inner] - inner_link * inner_link * thin[-1][-1],
        ),
        (top_link * top_link * panels[0][:size], top_link * top_link * thin[0][0]),
        (inner_link * top_link * panels[0][-size:], inner_link * top_link * thin[0][-1]),
    ]
    for k, (block, floor) in enumerate(blocks):
        send_ref[k, :size] = block
        send_ref[k, size:] = jnp.broadcast_to(floor, (8, size))


def interface(all_ref, ends_ref, high_ref, low_ref, rows_ref):
    count, size = all_ref.shape[0], all_ref.shape[3]

    def diag_of(rows, cols):
        own = [all_ref[k, 0, rows, cols] for k in range(count)]
        return [
            own[k] - all_ref[k + 1, 1, rows, cols] if k + 1 < count else own[k]
            for k in range(count)
        ]

    def low(k, x, transposed=False, right=False):
        block = all_ref[k, 2, :size]
        if right:
            return dot_t(x, block) if transposed else dot(x, block)
        return dot(block, x, ((0,), (0,))) if transposed else dot(block, x)

    thin = slice(size, size + 1), slice(0, 1)
    panels, _ = dense_inverse(
        diag_of(slice(0, size), slice(0, size)),
        low,
        diag_of(*thin),
        [all_ref[k, 2, thin[0], thin[1]] for k in range(count)],
        enough_steps(spread(size)),
    )
    for k, panel in enumerate(panels):
        rows_ref[k] = panel
    me = lax.axis_index("lev")
    own = rows_ref[me]
    above = rows_ref[jnp.maximum(me - 1, 0)]
    inner = dot_t(ends_ref[0], above) + dot_t(ends_ref[1], own)
    length = inner.shape[0]
    high_ref[:length], low_ref[:length] = split(inner)
    high_ref[length:], low_ref[length:] = split(own.T)


def send(src, dst, sems, slot, device):
    return pltpu.make_async_remote_copy(
        src_ref=src,
        dst_ref=dst,
        send_sem=sems.at[0, slot],
        recv_sem=sems.at[1, slot],
        device_id=device,
        device_id_type=pl.DeviceIdType.MESH,
    )


def greet(lev_all, lon_all):
    barrier = pltpu.get_barrier_semaphore()
    partners = []
    for axis, everyone in (("lev", lev_all), ("lon", lon_all)):
        count, me = lax.axis_size(axis), lax.axis_index(axis)
        if everyone is None:
            continue
        steps = range(1, count) if everyone else sorted({1, count - 1})
        partners += [{axis: lax.rem(me + d, count)} for d in steps if d % count]
    for device in partners:
        pl.semaphore_signal(
            barrier, inc=1, device_id=device, device_id_type=pl.DeviceIdType.MESH
        )
    pl.semaphore_wait(barrier, len(partners))


def pack_edges(cur_ref, edges_ref):
    levels, size, columns = cur_ref.shape
    lane = lax.broadcasted_iota(jnp.int32, (size, 128), 1)
    last = jnp.zeros((size, 128), jnp.float32)
    first = last
    for k in range(levels):
        tail = pltpu.roll(cur_ref[k, :, columns - 128 :], k + 1, 1)
        head = cur_ref[k, :, :128]
        head = pltpu.roll(head, k, 1) if k else head
        last = jnp.where(lane == k, tail, last)
        first = jnp.where(lane == k, head, first)
    edges_ref[0] = last
    edges_ref[1] = first


def halo_copies(edges_ref, halo_ref, sems):
    around, me = lax.axis_size("lon"), lax.axis_index("lon")
    return [
        send(edges_ref.at[0], halo_ref.at[0], sems, 0, {"lon": lax.rem(me + 1, around)}),
        send(edges_ref.at[1], halo_ref.at[1], sems, 1, {"lon": lax.rem(me + around - 1, around)}),
    ]


def local_forcing(mix_ref, cur_ref, prev_ref, pair_ref, force_ref):
    levels, size, columns = cur_ref.shape
    lane = lax.broadcasted_iota(jnp.int32, (size, columns), 1)
    for k in range(levels):
        c = cur_ref[k]
        back = jnp.where(lane == 0, 0.0, pltpu.roll(c, 1, 1))
        ahead = jnp.where(lane == columns - 1, 0.0, pltpu.roll(c, columns - 1, 1))
        p_high, p_low = split(pair_ref[k])
        chem = dot3(p_high, p_low, c * c)
        force_ref[k * size : (k + 1) * size] = (
            prev_ref[k] - chem + mix_ref[k] * (back + ahead - 2.0 * c)
        )


def add_halo(mix_ref, halo_ref, force_ref):
    levels = mix_ref.shape[0]
    size, columns = halo_ref.shape[1], force_ref.shape[1]
    lane = lax.broadcasted_iota(jnp.int32, (size, 128), 1)
    before, after = halo_ref[0], halo_ref[1]
    for k in range(levels):
        rows = slice(k * size, (k + 1) * size)
        at_head = pltpu.roll(before, 128 - k, 1) if k else before
        at_tail = pltpu.roll(after, 127 - k, 1)
        force_ref[rows, :128] += jnp.where(lane == 0, mix_ref[k] * at_head, 0.0)
        force_ref[rows, columns - 128 :] += jnp.where(lane == 127, mix_ref[k] * at_tail, 0.0)


def couple(
    links_ref, top_link, g_high, g_low, force_ref, part_ref, f_high, f_low, top_out, top_in, sides_ref,
    sems, direct,
):
    count, me = lax.axis_size("lev"), lax.axis_index("lev")
    inner, size = part_ref.shape[0], top_out.shape[0]
    f_high[...], f_low[...] = split(force_ref[:inner])
    mul = functools.partial(jnp.dot, preferred_element_type=jnp.float32)

    def rows_of(start, stop):
        a, b = g_high[start:stop], g_low[start:stop]
        part = mul(a, f_high[...]) + (mul(b, f_high[...]) + mul(a, f_low[...]))
        part_ref[start:stop] = part
        return part

    top_out[...] = top_link * rows_of(0, size)
    sides_ref[me] = force_ref[inner:] + links_ref[inner // size - 1] * rows_of(inner - size, inner)
    up = send(top_out, top_in, sems, 0, {"lev": lax.rem(me + count - 1, count)})
    half = size * ((inner // size) // 2)

    @pl.when(me > 0)
    def _():
        up.start()

    rows_of(size, half)

    @pl.when(me < count - 1)
    def _():
        up.wait_recv()
        sides_ref[me] += top_in[...]

    partner = me + 1 - 2 * lax.rem(me, 2)
    copies = [
        send(sides_ref.at[me], sides_ref.at[me], sems, d, {"lev": lax.rem(me + d, count)})
        for d in range(1 if direct else 2, count, 1 if direct else 2)
    ]
    onward = [] if direct else [send(sides_ref.at[me], sides_ref.at[me], sems, 1, {"lev": partner})]
    for d in range(count if direct else 2, count, 2):
        origin = lax.rem(me - d + count, count)
        onward.append(
            send(sides_ref.at[origin], sides_ref.at[origin], sems, d + 1, {"lev": partner})
        )
    for copy in copies + onward[:1]:
        copy.start()
    rows_of(half, inner - size)

    @pl.when(me > 0)
    def _():
        up.wait_send()

    return copies, onward


def relay(copies, onward):
    for copy, later in zip(copies, onward[1:]):
        copy.wait_recv()
        later.start()
    for copy in copies:
        copy.wait_send()
    for copy in onward:
        copy.wait()


def finish(part_ref, sides_ref, high_ref, low_ref, out_ref):
    levels, size, columns = out_ref.shape
    count = sides_ref.shape[0]
    b_high, b_low = split(sides_ref[...].reshape(count * size, columns))
    mul = functools.partial(jnp.dot, preferred_element_type=jnp.float32)
    for k in range(levels):
        rows = slice(k * size, (k + 1) * size)
        a, b = high_ref[rows], low_ref[rows]
        row = mul(a, b_high) + (mul(b, b_high) + mul(a, b_low))
        out_ref[k] = row + part_ref[rows] if k < levels - 1 else row


def open_kernel(
    links_ref, mix_ref, prev_ref, pair_ref, force_ref, top_ref, edges, halo, link_out, sems
):
    levels = prev_ref.shape[0]
    count, me = lax.axis_size("lev"), lax.axis_index("lev")
    pack_edges(prev_ref, edges)
    link_out[...] = jnp.full(link_out.shape, links_ref[levels - 1], jnp.float32)
    greet(False, False)
    copies = halo_copies(edges, halo, sems)
    down = send(link_out, top_ref, sems, 2, {"lev": lax.rem(me + 1, count)})
    for copy in copies:
        copy.start()

    @pl.when(me < count - 1)
    def _():
        down.start()

    @pl.when(me == 0)
    def _():
        top_ref[...] = jnp.zeros(top_ref.shape, jnp.float32)

    local_forcing(mix_ref, prev_ref, prev_ref, pair_ref, force_ref)
    for copy in copies:
        copy.wait()
    add_halo(mix_ref, halo, force_ref)

    @pl.when(me < count - 1)
    def _():
        down.wait_send()

    @pl.when(me > 0)
    def _():
        down.wait_recv()


def newton_kernel(
    links_ref, mix_ref, top_ref, sent_ref, ends_ref, first_force, g_high, g_low, prev_ref, pair_ref,
    out_ref, var_ref, all_ref, rows_ref, h_high, h_low, cur_ref, edges, halo, force_ref, part_ref,
    first_sides, sides_ref, f_high, f_low, first_out, first_in, top_out, top_in, sums_ref,
    block_sems, first_sems, halo_sems, sems, sum_sems,
):
    levels, size, columns = prev_ref.shape
    count, me = lax.axis_size("lev"), lax.axis_index("lev")
    around, place = lax.axis_size("lon"), lax.axis_index("lon")
    greet(True, True)
    blocks = [
        send(sent_ref, all_ref.at[me], block_sems, d, {"lev": lax.rem(me + d, count)})
        for d in range(1, count)
    ]
    for copy in blocks:
        copy.start()
    all_ref[me] = sent_ref[...]
    copies = couple(
        links_ref, top_ref[0:1, 0:1], g_high, g_low, first_force, part_ref, f_high, f_low,
        first_out, first_in, first_sides, first_sems, True,
    )
    for copy in blocks:
        copy.wait()
    interface(all_ref, ends_ref, h_high, h_low, rows_ref)
    for copy in copies[0]:
        copy.wait()
    finish(part_ref, first_sides, h_high, h_low, cur_ref)
    pack_edges(cur_ref, edges)
    copies = halo_copies(edges, halo, halo_sems)
    for copy in copies:
        copy.start()
    local_forcing(mix_ref, cur_ref, prev_ref, pair_ref, force_ref)
    for copy in copies:
        copy.wait()
    add_halo(mix_ref, halo, force_ref)
    copies = couple(
        links_ref, top_ref[0:1, 0:1], g_high, g_low, force_ref, part_ref, f_high, f_low,
        top_out, top_in, sides_ref, sems, False,
    )
    relay(*copies)
    finish(part_ref, sides_ref, h_high, h_low, out_ref)
    lane = lax.broadcasted_iota(jnp.int32, (size, 128), 1)
    total = jnp.zeros((size, 128), jnp.float32)
    for k in range(levels):
        row = out_ref[k]
        total = jnp.where(lane == k, jnp.sum(row * row, axis=1, keepdims=True), total)
    sums_ref[0] = total.T[: sums_ref.shape[1]]
    copies = [
        send(sums_ref.at[0], sums_ref.at[d], sum_sems, d, {"lon": lax.rem(place + d, around)})
        for d in range(1, around)
    ]
    for copy in copies:
        copy.start()
    for copy in copies:
        copy.wait()
    total = sums_ref[place]
    for j in range(1, around):
        total = total + sums_ref[lax.rem(place - j + around, around)]
    var_ref[...] = (total / (columns * around))[:levels]


def call(kernel, outs, places, scratch=(), group=None):
    extra = {} if group is None else {"collective_id": group, "has_side_effects": True}
    return pl.pallas_call(
        kernel,
        out_shape=[jax.ShapeDtypeStruct(shape, dtype) for shape, dtype in outs],
        in_specs=places,
        out_specs=[VMEM] * len(outs),
        scratch_shapes=list(scratch),
        compiler_params=pltpu.CompilerParams(vmem_limit_bytes=60 * 2**20, **extra),
    )


def local(previous, loss_matrix, pair_matrix, diffusivity, mixing):
    levels, size, columns = previous.shape
    count = lax.axis_size("lev")
    around = lax.axis_size("lon")
    inner = (levels - 1) * size
    f32, bf16 = jnp.float32, jnp.bfloat16
    buf, sem = pltpu.VMEM, lambda n: pltpu.SemaphoreType.DMA((2, n))
    force, top = call(
        open_kernel,
        [((levels * size, columns), f32), ((8, 128), f32)],
        [SMEM, SMEM, VMEM, VMEM],
        [buf((2, size, 128), f32), buf((2, size, 128), f32), buf((8, 128), f32), sem(3)],
        0,
    )(diffusivity, mixing, previous, pair_matrix)
    g_high, g_low, ends, sent = call(
        factor_kernel,
        [((inner, inner), bf16), ((inner, inner), bf16), ((2, inner, size), f32), ((3, size + 8, size), f32)],
        [SMEM, VMEM, VMEM],
    )(diffusivity, top, loss_matrix)
    return call(
        newton_kernel,
        [((levels, size, columns), f32), ((levels, size), f32)],
        [SMEM, SMEM] + [VMEM] * 8,
        [
            buf((count, 3, size + 8, size), f32),
            buf((count, count * size, size), f32),
            buf((levels * size, count * size), bf16),
            buf((levels * size, count * size), bf16),
            buf((levels, size, columns), f32),
            buf((2, size, 128), f32),
            buf((2, size, 128), f32),
            buf((levels * size, columns), f32),
            buf((inner, columns), f32),
            buf((count, size, columns), f32),
            buf((count, size, columns), f32),
            buf((inner, columns), bf16),
            buf((inner, columns), bf16),
            buf((size, columns), f32),
            buf((size, columns), f32),
            buf((size, columns), f32),
            buf((size, columns), f32),
            buf((around, -(-levels // 8) * 8, size), f32),
            sem(count),
            sem(count),
            sem(2),
            sem(count),
            sem(around),
        ],
        1,
    )(diffusivity, mixing, top, sent, ends, force, g_high, g_low, previous, pair_matrix)


def solution(mesh):
    placed = (P("lev", None, "lon"), P("lev", None, None), P("lev", None, None), P("lev"), P("lev"))
    return jax.shard_map(
        local,
        mesh=mesh,
        in_specs=placed,
        out_specs=(P("lev", None, "lon"), P("lev", None)),
        check_vma=False,
    )
```

profile of v0, /device:TPU:0, one launch (start us, length us, event | category | flops | bytes accessed | tf_op | source)
XLA Modules:
  0.0 71.6 jit_solution(5210332782697722564)
XLA Ops:
  0.6 12.0 %shard_map.68 = (f32[576,512]{1,0:T(8,128)}, f32[8,128]{1,0:T(8,128)}) custom-call(f32[9]{0:T(128)} %links_ref.5, f32[9]{0:T(128)} %mix_ref.3, f32[9,64,512]{2,1,0:T(8,128)} %prev_ref.3, f32[9,64,64]{2,1,0:T(8,128)} %pair_ref.3), custom_call_target="tpu_custom_call" | custom-call | tf_op jit(solution)/shard_map/pallas_call | solution.py:497
  12.7 9.8 %shard_map.69 = (bf16[512,512]{1,0:T(8,128)(2,1)}, bf16[512,512]{1,0:T(8,128)(2,1)}, f32[2,512,64]{2,1,0:T(8,128)}, f32[3,72,64]{2,1,0:T(8,128)}) custom-call(f32[9]{0:T(128)} %links_ref.5, f32[8,128]{1,0:T(8,128)} %get-tuple-element.8.top_ref, f32[9,64,64]{2,1,0:T(8,128)} %loss_ref.1), custom_call_target="tpu_custom_call" | custom-call | tf_op jit(solution)/shard_map/pallas_call | solution.py:504
  22.5 46.1 %shard_map.70 = (f32[9,64,512]{2,1,0:T(8,128)}, f32[9,64]{1,0:T(8,128)}) custom-call(f32[9]{0:T(128)} %links_ref.5, f32[9]{0:T(128)} %mix_ref.3, f32[8,128]{1,0:T(8,128)} %get-tuple-element.8.top_ref, f32[3,72,64]{2,1,0:T(8,128)} %get-tuple-element.9.sent_ref, f32[2,512,64]{2,1,0:T(8,128)} %get-tuple-element.10.ends_ref, ...), custom_call_target="tpu_custom_call" | custom-call | tf_op jit(solution)/shard_map/pallas_call | solution.py:509
  68.6 0.0 copy-start
  68.6 2.4 %copy.9 = f32[9,64,512]{2,1,0:T(8,128)} copy(f32[9,64,512]{2,1,0:T(8,128)} %get-tuple-element.16) | data formatting | bytes 2359296
  71.0 0.0 copy-done
  71.0 0.6 copy.10
Async XLA Ops:
  68.6 2.4 %copy-start = (f32[9,64]{1,0:T(8,128)S(1)}, f32[9,64]{1,0:T(8,128)}, u32[]{:S(2)}) copy-start(f32[9,64]{1,0:T(8,128)} %get-tuple-element.17) | copy-start | bytes 6916
where the time goes:
time: 71.5 us; the launch traced here: 71.6 us
  Pallas kernels  68 us (95%)
  local copies, waits for them, and re-layouts  2.97 us (4%)
    pallas_call x1, Pallas kernels, local(): call(newton_kernel, [((levels, size, columns), f32), ((levels, size), f32...  46.1 us
    pallas_call x1, Pallas kernels, local(): call(open_kernel, [((levels * size, columns), f32), ((8, 128), f32)], [SM...  12 us
    pallas_call x1, Pallas kernels, local(): call(factor_kernel, [((inner, inner), bf16), ((inner, inner), bf16), ((2,...  9.81 us
    unnamed x4, local copies, waits for them, and re-layouts  2.97 us

commit v1 on v0

--- a/solution.py
+++ b/solution.py
@@ -1,4 +1,5 @@
 import functools
+import itertools
 
 import jax
 import jax.numpy as jnp
@@ -539,10 +540,499 @@
     )(diffusivity, mixing, top, sent, ends, force, g_high, g_low, previous, pair_matrix)
 
 
+def cat3(a_high, a_low, b_high, b_low):
+    return jnp.dot(
+        jnp.concatenate([a_high, a_low, a_high], axis=1),
+        jnp.concatenate([b_high, b_high, b_low], axis=0),
+        preferred_element_type=jnp.float32,
+    )
+
+
+def wide(a):
+    high, low = split(a)
+    return jnp.concatenate([high, low, high, jnp.zeros_like(high)], axis=1)
+
+
+def tall(b):
+    high, low = split(b)
+    return jnp.concatenate([high, high, low, jnp.zeros_like(high)], axis=0)
+
+
+def wide_dot(a, b):
+    return jnp.dot(a, b, preferred_element_type=jnp.float32)
+
+
+def pull(links, loss):
+    stiff = links[0]
+    for a in links[1:]:
+        own = 1.0 + loss + stiff
+        stiff = a * own / (a + own)
+    return stiff
+
+
+def worst_ratio(above, below):
+    sides = []
+    for count in (above, below):
+        draws = itertools.product((200.0, 2000.0), repeat=min(count, 8) + 1)
+        sides.append([(pull(d, 640.0), pull(d, 0.05)) for d in draws])
+    return 1.15 * max((641.0 + a + c) / (1.05 + b + d) for a, b in sides[0] for c, d in sides[1])
+
+
+def gains_for(ratio):
+    rho, gains = (ratio - 1.0) / (ratio + 1.0), []
+    while rho > 1.5e-4:
+        gains.append(2.0 / (2.0 - rho * rho))
+        rho = rho * rho / (2.0 - rho * rho)
+    return gains
+
+
+def invert_fixed(blocks, floors, ratio):
+    size = blocks[0].shape[0]
+    unit = jnp.where(eye_of(size), 1.0, 0.0).astype(jnp.float32)
+    gains = gains_for(ratio)
+    xs, rests = [], []
+    for a, low in zip(blocks, floors):
+        scale = (2.0 / (1.0 + ratio)) / low
+        rest = unit - scale * a
+        xs.append((gains[0] * scale) * (unit + rest))
+        rests.append(rest)
+    rests = [gains[0] * dot(r, r) - (gains[0] - 1.0) * unit for r in rests]
+    for step, g in enumerate(gains[1:]):
+        if step + 2 == len(gains):
+            xs = [g * (x + dot(x, r)) for x, r in zip(xs, rests)]
+            break
+        both = [dot(jnp.concatenate([x, r], axis=0), r) for x, r in zip(xs, rests)]
+        xs = [g * (x + b[:size]) for x, b in zip(xs, both)]
+        rests = [g * b[size:] - (g - 1.0) * unit for b in both]
+    rests = [unit - dot(a, x) for a, x in zip(blocks, xs)]
+    return [x + dot(x, r) for x, r in zip(xs, rests)]
+
+
+def chain_factor(diag, links, floors, panel_ref, hook):
+    count, size = len(diag), diag[0].shape[0]
+    unit = jnp.where(eye_of(size), 1.0, 0.0).astype(jnp.float32)
+    by_depth, thin = {}, {}
+    plan(0, count, by_depth)
+
+    def rows(lo, hi):
+        return slice(lo * size, hi * size)
+
+    for depth in sorted(by_depth):
+        nodes = by_depth[depth]
+        ratio = max(worst_ratio(mid - lo, hi - 1 - mid) for lo, mid, hi in nodes)
+        schur, arms, lows, thin_arms = [], [], [], []
+        for lo, mid, hi in nodes:
+            s, parts = diag[mid], []
+            t, thin_parts = floors[mid], []
+            if lo < mid:
+                arm = links[mid] * panel_ref[mid - 1, rows(lo, mid)]
+                s = s - links[mid] * arm[-size:]
+                parts.append(arm)
+                thin_parts += [links[mid] * x for x in thin[lo, mid][-1]]
+                t = t - links[mid] * thin_parts[-1]
+            parts.append(unit)
+            thin_parts.append(1.0)
+            if mid + 1 < hi:
+                arm = links[mid + 1] * panel_ref[mid + 1, rows(mid + 1, hi)]
+                s = s - links[mid + 1] * arm[:size]
+                parts.append(arm)
+                thin_arm = [links[mid + 1] * x for x in thin[mid + 1, hi][0]]
+                t = t - links[mid + 1] * thin_arm[0]
+                thin_parts += thin_arm
+            schur.append(s)
+            lows.append(t)
+            arms.append(jnp.concatenate(parts, axis=0) if len(parts) > 1 else parts[0])
+            thin_arms.append(thin_parts)
+        inverses = invert_fixed(schur, [0.97 * t for t in lows], ratio)
+        for (lo, mid, hi), v, z, thin_v, t in zip(nodes, arms, inverses, thin_arms, lows):
+            thin[lo, hi] = [[a * b / t for b in thin_v] for a in thin_v]
+            for a, b in ((lo, mid), (mid + 1, hi)):
+                for i in range(a, b):
+                    for j in range(a, b):
+                        thin[lo, hi][i - lo][j - lo] += thin[a, b][i - a][j - a]
+            if hi - lo == 1:
+                panel_ref[mid, rows(mid, hi)] = z
+                continue
+            w = dot(v, z)
+            if hi - lo == count:
+                continue
+            new = dot_t(w, v)
+            for k in range(lo, hi):
+                own = new[:, (k - lo) * size : (k - lo + 1) * size]
+                panel_ref[k, rows(mid, mid + 1)] = own[rows(mid - lo, mid - lo + 1)]
+                for a, b in ((lo, mid), (mid + 1, hi)):
+                    if a >= b:
+                        continue
+                    piece = own[rows(a - lo, b - lo)]
+                    if a <= k < b:
+                        piece = piece + panel_ref[k, rows(a, b)]
+                    panel_ref[k, rows(a, b)] = piece
+        if depth < max(by_depth):
+            hook(depth)
+    return v, w, by_depth[max(by_depth)][0][1], thin[0, count]
+
+
+def fold(x):
+    half = x.shape[0] // 2
+    return jnp.concatenate([x[:half], x[half:]], axis=1)
+
+
+def unfold(x):
+    half = x.shape[1] // 2
+    return jnp.concatenate([x[:, :half], x[:, half:]], axis=0)
+
+
+def pack_pairs(field_ref, columns, edges_ref):
+    levels, size = field_ref.shape[:2]
+    lane = lax.broadcasted_iota(jnp.int32, (size, 128), 1)
+    last = jnp.zeros((size, 128), jnp.float32)
+    first = last
+    for k in range(levels):
+        tail = pltpu.roll(field_ref[k, :, columns - 128 : columns], (2 * k + 2) % 128, 1)
+        head = field_ref[k, :, :128]
+        head = pltpu.roll(head, 2 * k, 1) if k else head
+        mine = (lane == 2 * k) | (lane == 2 * k + 1)
+        last = jnp.where(mine, tail, last)
+        first = jnp.where(mine, head, first)
+    edges_ref[0] = last
+    edges_ref[1] = first
+
+
+def unpack_pairs(halo_ref, columns, field_ref):
+    levels, size = field_ref.shape[:2]
+    lane = lax.broadcasted_iota(jnp.int32, (size, 128), 1)
+    before, after = halo_ref[0], halo_ref[1]
+    for k in range(levels):
+        at_head = pltpu.roll(after, (128 - 2 * k) % 128, 1) if k else after
+        at_tail = pltpu.roll(before, (126 - 2 * k) % 128, 1)
+        field_ref[k, :, columns:] = jnp.where(lane < 2, at_head, jnp.where(lane >= 126, at_tail, 0.0))
+
+
+def forcing(mix_ref, cur_ref, prev_ref, pairs_ref, width, sep_ref, f_high, f_low):
+    levels, size, full = cur_ref.shape
+    for k in range(levels):
+        c = cur_ref[k]
+        ring = pltpu.roll(c, 1, 1) + pltpu.roll(c, full - 1, 1)
+        own = c[:, :width]
+        chem = wide_dot(pairs_ref[k], tall(own * own))
+        force = prev_ref[k, :, :width] - chem + mix_ref[k] * (ring[:, :width] - 2.0 * own)
+        if k == 0:
+            sep_ref[:, :width] = force
+        else:
+            rows = slice((k - 1) * size, k * size)
+            f_high[rows, :width], f_low[rows, :width] = split(force)
+
+
+def start_all(copies):
+    @pl.when(lax.axis_index("lev") < lax.axis_size("lev"))
+    def _():
+        for copy in copies:
+            copy.start()
+
+
+def step_kernel(
+    links_ref, mix_ref, loss_hbm, prev_hbm, pair_hbm, out_ref, var_ref,
+    loss_ref, prev_ref, pair_ref, pairs_ref, edges, halo, z_high, z_low, send_ref, all_ref,
+    ends_high, ends_low, table_ref, sep_ref, f_high, f_low, part_ref, own_ref, near_ref, mine_ref, far_ref,
+    side_high, side_low, hq_high, hq_low, u_ref, top_ref, cur_ref, sums_ref, panel_ref,
+    load_sems, halo_sems, block_sems, near_sems, far_sems, sum_sems,
+):
+    levels, size, columns = prev_hbm.shape
+    inner = levels - 1
+    full = cur_ref.shape[2]
+    count, me = lax.axis_size("lev"), lax.axis_index("lev")
+    around, place = lax.axis_size("lon"), lax.axis_index("lon")
+    core, chip = lax.rem(me, 2), me // 2
+    partner = me + 1 - 2 * core
+    across = lax.rem(me + 2, count)
+
+    loads = [
+        pltpu.make_async_copy(loss_hbm, loss_ref, load_sems.at[0]),
+        pltpu.make_async_copy(prev_hbm, prev_ref.at[:, :, pl.ds(0, columns)], load_sems.at[1]),
+        pltpu.make_async_copy(pair_hbm, pair_ref, load_sems.at[2]),
+    ]
+    for load in loads:
+        load.start()
+    barrier = pltpu.get_barrier_semaphore()
+    partners = [{"lev": lax.rem(me + d, count)} for d in range(1, count)]
+    partners += [{"lon": lax.rem(place + d, around)} for d in range(1, around)]
+    for device in partners:
+        pl.semaphore_signal(barrier, inc=1, device_id=device, device_id_type=pl.DeviceIdType.MESH)
+
+    links = [jnp.full((1, 1), links_ref[k]) for k in range(levels)]
+    on_diag = eye_of(size)
+    halo_moves = halo_copies(edges, halo, halo_sems)
+
+    def hook(depth):
+        if depth != 2:
+            return
+        loads[1].wait()
+        pack_pairs(prev_ref, columns, edges)
+        pl.semaphore_wait(barrier, len(partners))
+        start_all(halo_moves)
+
+    loads[0].wait()
+    diag = [
+        loss_ref[k] + jnp.where(on_diag, 1.0 + links[k] + (links[k - 1] if k else 0.0), 0.0)
+        for k in range(levels)
+    ]
+    floors = [LEAST + links[k] + (links[k - 1] if k else 0.0) for k in range(levels)]
+    v, w, mid, thin = chain_factor(diag[1:], links[:inner], floors[1:], panel_ref, hook)
+    a, b = links[0], links[inner]
+    old = [
+        panel_ref[0, : mid * size],
+        jnp.zeros((size, size), jnp.float32),
+        panel_ref[inner - 1, (mid + 1) * size :],
+    ]
+    tips = dot_t(w, jnp.concatenate([v[:size], v[-size:]], axis=0))
+    first = tips[:, :size] + jnp.concatenate([old[0], old[1], jnp.zeros_like(old[2])], axis=0)
+    last = tips[:, size:] + jnp.concatenate([jnp.zeros_like(old[0]), old[1], old[2]], axis=0)
+    sub = lax.broadcasted_iota(jnp.int32, (8, 128), 0)
+    send_ref[: size // 2] = fold(diag[0] - a * a * first[:size])
+    send_ref[size // 2 : size] = fold(jnp.where(on_diag, b, 0.0) - b * b * last[-size:])
+    send_ref[size : 3 * size // 2] = fold(a * b * first[-size:])
+    send_ref[3 * size // 2 :] = jnp.where(
+        sub == 0, floors[0] - a * a * thin[0][0], jnp.where(sub == 1, b - b * b * thin[-1][-1], a * b * thin[0][-1])
+    )
+    blocks = [
+        send(send_ref, all_ref.at[me], block_sems, d, {"lev": lax.rem(me + d, count)})
+        for d in range(1, count)
+    ]
+    start_all(blocks)
+    all_ref[me] = send_ref[...]
+
+    ends_high[...], ends_low[...] = split(jnp.concatenate([a * first, b * last], axis=1))
+    w_wide, (v_high, v_low) = wide(w), split(v)
+    v_wide = jnp.concatenate([v_high, v_high, v_low, jnp.zeros_like(v_high)], axis=1)
+    for k in range(0, inner, 2):
+        new = lax.dot_general(
+            w_wide, v_wide[k * size : (k + 2) * size], (((1,), (1,)), ((), ())), preferred_element_type=jnp.float32
+        )
+        for lo, hi in ((0, mid), (mid, mid + 1), (mid + 1, inner)):
+            piece = new[lo * size : hi * size]
+            if lo != mid and (lo <= k < hi or lo <= k + 1 < hi):
+                old = [
+                    panel_ref[j, lo * size : hi * size] if lo <= j < hi else jnp.zeros((piece.shape[0], size), jnp.float32)
+                    for j in (k, k + 1)
+                ]
+                piece = piece + jnp.concatenate(old, axis=1)
+            spot = slice(lo * size, hi * size), slice(k * size, (k + 2) * size)
+            z_high[spot], z_low[spot] = split(piece)
+    loads[2].wait()
+    for k in range(levels):
+        pairs_ref[k] = wide(pair_ref[k])
+    for move in halo_moves:
+        move.wait()
+    unpack_pairs(halo, columns, prev_ref)
+
+    def z_rows(start, stop, width):
+        return cat3(z_high[start:stop], z_low[start:stop], f_high[:, :width], f_low[:, :width])
+
+    def ends(turn, width):
+        rows = cat3(
+            jnp.concatenate([z_high[:size], z_high[-size:]], axis=0),
+            jnp.concatenate([z_low[:size], z_low[-size:]], axis=0),
+            f_high[:, :width],
+            f_low[:, :width],
+        )
+        part_ref[:size, :width] = rows[:size]
+        part_ref[-size:, :width] = rows[size:]
+        own_ref[turn, 0, :, :width] = sep_ref[:, :width] + a * rows[:size]
+        own_ref[turn, 1, :, :width] = b * rows[size:]
+        copy = send(
+            own_ref.at[turn, :, :, pl.ds(0, width)], near_ref.at[turn, :, :, pl.ds(0, width)], near_sems, turn,
+            {"lev": partner},
+        )
+        start_all([copy])
+        return copy
+
+    def middle(width):
+        for k in range(1, inner - 1):
+            part_ref[k * size : (k + 1) * size, :width] = z_rows(k * size, (k + 1) * size, width)
+
+    def merge(turn, width):
+        upper = core == 0
+        s_own, t_own = own_ref[turn, 0, :, :width], own_ref[turn, 1, :, :width]
+        s_in, t_in = near_ref[turn, 0, :, :width], near_ref[turn, 1, :, :width]
+        low_side = jnp.where(upper, s_own, s_in)
+        high_side = jnp.where(upper, s_in + t_own, s_own + t_in)
+        side_high[:size, :width], side_low[:size, :width] = split(low_side)
+        side_high[size:, :width], side_low[size:, :width] = split(high_side)
+        return jnp.where(chip == 0, jnp.where(upper, t_in, t_own), 0.0)
+
+    def condense(turn, width, tail, k_high, k_low):
+        mine_ref[turn, :, :width] = tail + cat3(k_high, k_low, side_high[:, :width], side_low[:, :width])
+        copy = send(
+            mine_ref.at[turn, :, pl.ds(0, width)], far_ref.at[turn, :, pl.ds(0, width)], far_sems, turn,
+            {"lev": across},
+        )
+        start_all([copy])
+        return copy
+
+    def gather_sides(width):
+        for k in range(levels):
+            spot = slice(k * size, (k + 1) * size)
+            rows = cat3(hq_high[spot], hq_low[spot], side_high[:, :width], side_low[:, :width])
+            cur_ref[k, :, :width] = rows if k == 0 else rows + part_ref[(k - 1) * size : k * size, :width]
+
+    def finish(turn, width, to_ref):
+        total = mine_ref[turn, :, :width] + far_ref[turn, :, :width]
+        top = tall(wide_dot(top_ref[...], tall(total)))
+        for k in range(levels):
+            to_ref[k, :, :width] = cur_ref[k, :, :width] + wide_dot(u_ref[k * size : (k + 1) * size], top)
+
+    forcing(mix_ref, prev_ref, prev_ref, pairs_ref, full, sep_ref, f_high, f_low)
+    near = ends(0, full)
+    middle(full)
+    for copy in blocks:
+        copy.wait()
+
+    def block(k, which):
+        return unfold(all_ref[k, which * size // 2 : (which + 1) * size // 2])
+
+    def floor(k, which):
+        row = 3 * size // 2 + which
+        return all_ref[k, row : row + 1, 0:1]
+
+    ratio = spread(size)
+    s = [block(k, 0) + (block(k - 1, 1) if k else 0.0) for k in range(count)]
+    t = [floor(k, 0) + (floor(k - 1, 1) if k else 0.0) for k in range(count)]
+    c = [None] + [block(k, 2) for k in range(count - 1)]
+    e = [None] + [floor(k, 2) for k in range(count - 1)]
+    z0, z3 = invert_fixed([s[0], s[3]], [0.97 * t[0], 0.97 * t[3]], ratio)
+    a1, a3 = dot(c[1], z0), dot(z3, c[3])
+    s1 = s[1] - dot_t(a1, c[1])
+    t1 = t[1] - e[1] * e[1] / t[0]
+    (z1,) = invert_fixed([s1], [0.97 * t1], ratio)
+    a2 = dot(c[2], z1)
+    s2 = s[2] - dot_t(a2, c[2]) - dot(c[3], a3, ((0,), (0,)))
+    t2 = t[2] - e[2] * e[2] / t1 - e[3] * e[3] / t[3]
+    b1 = dot(z1, a1)
+    p0 = dot(a2, a1)
+    zero = jnp.zeros((size, size), jnp.float32)
+    unit = jnp.where(on_diag, 1.0, 0.0).astype(jnp.float32)
+    sides = [
+        (z0 + dot(a1, b1, ((0,), (0,))), b1.T, p0.T),
+        (b1, z1, a2.T),
+        (zero, zero, unit),
+        (zero, z3, a3),
+        (zero, zero, zero),
+    ]
+    for k, (left, right, top) in enumerate(sides):
+        table_ref[k, :size] = jnp.concatenate([left, right], axis=1)
+        table_ref[k, size:, :size] = top
+    for k, (left, right) in enumerate(((p0, a2), (unit, a3.T))):
+        table_ref[len(sides) + k, :size] = jnp.concatenate([left, right], axis=1)
+    near.wait()
+    tail = merge(0, full)
+    k_high, k_low = split(table_ref[len(sides) + chip, :size])
+    far = condense(0, full, tail, k_high, k_low)
+    (z2,) = invert_fixed([s2], [0.97 * t2], ratio)
+    top_ref[...] = wide(z2)
+    own_q, next_q = table_ref[me, :size], table_ref[me + 1, :size]
+    own_p, next_p = table_ref[me, size:, :size], table_ref[me + 1, size:, :size]
+    q_high, q_low = split(jnp.concatenate([own_q, next_q], axis=0))
+    p_high, p_low = split(jnp.concatenate([own_p, next_p], axis=0))
+    hq_high[size:], hq_low[size:] = split(cat3(ends_high[...], ends_low[...], q_high, q_low))
+    hq_high[:size], hq_low[:size] = split(own_q)
+    u_ref[size:] = wide(cat3(ends_high[...], ends_low[...], p_high, p_low))
+    u_ref[:size] = wide(own_p)
+    gather_sides(full)
+    far.wait()
+    finish(0, full, cur_ref)
+
+    forcing(mix_ref, cur_ref, prev_ref, pairs_ref, columns, sep_ref, f_high, f_low)
+    near = ends(1, columns)
+    middle(columns)
+    near.wait()
+    tail = merge(1, columns)
+    far = condense(1, columns, tail, k_high, k_low)
+    gather_sides(columns)
+    far.wait()
+    finish(1, columns, out_ref)
+    lane = lax.broadcasted_iota(jnp.int32, (size, 128), 1)
+    total = jnp.zeros((size, 128), jnp.float32)
+    for k in range(levels):
+        row = out_ref[k]
+        total = jnp.where(lane == k, jnp.sum(row * row, axis=1, keepdims=True), total)
+    sums_ref[0] = total.T[: sums_ref.shape[1]]
+    copies = [
+        send(sums_ref.at[0], sums_ref.at[d], sum_sems, d, {"lon": lax.rem(place + d, around)})
+        for d in range(1, around)
+    ]
+    start_all(copies)
+    for copy in copies:
+        copy.wait()
+    total = sums_ref[place]
+    for j in range(1, around):
+        total = total + sums_ref[lax.rem(place - j + around, around)]
+    var_ref[...] = (total / (columns * around))[:levels]
+
+
+def local_pairs(previous, loss_matrix, pair_matrix, diffusivity, mixing):
+    levels, size, columns = previous.shape
+    count, around = lax.axis_size("lev"), lax.axis_size("lon")
+    inner, full = (levels - 1) * size, columns + 128
+    f32, bf16 = jnp.float32, jnp.bfloat16
+    buf, sem = pltpu.VMEM, lambda n: pltpu.SemaphoreType.DMA((2, n))
+    hbm = pl.BlockSpec(memory_space=pltpu.MemorySpace.HBM)
+    packed = 3 * size // 2 + 8
+    return pl.pallas_call(
+        step_kernel,
+        out_shape=[
+            jax.ShapeDtypeStruct((levels, size, columns), f32),
+            jax.ShapeDtypeStruct((levels, size), f32),
+        ],
+        in_specs=[SMEM, SMEM, hbm, hbm, hbm],
+        out_specs=[VMEM, VMEM],
+        scratch_shapes=[
+            buf((levels, size, size), f32),
+            buf((levels, size, full), f32),
+            buf((levels, size, size), f32),
+            buf((levels, size, 4 * size), bf16),
+            buf((2, size, 128), f32),
+            buf((2, size, 128), f32),
+            buf((inner, inner), bf16),
+            buf((inner, inner), bf16),
+            buf((packed, 2 * size), f32),
+            buf((count, packed, 2 * size), f32),
+            buf((inner, 2 * size), bf16),
+            buf((inner, 2 * size), bf16),
+            buf((count + 3, 2 * size, 2 * size), f32),
+            buf((size, full), f32),
+            buf((inner, full), bf16),
+            buf((inner, full), bf16),
+            buf((inner, full), f32),
+            buf((2, 2, size, full), f32),
+            buf((2, 2, size, full), f32),
+            buf((2, size, full), f32),
+            buf((2, size, full), f32),
+            buf((2 * size, full), bf16),
+            buf((2 * size, full), bf16),
+            buf((levels * size, 2 * size), bf16),
+            buf((levels * size, 2 * size), bf16),
+            buf((levels * size, 4 * size), bf16),
+            buf((size, 4 * size), bf16),
+            buf((levels, size, full), f32),
+            buf((around, -(-levels // 8) * 8, size), f32),
+            buf((levels - 1, inner, size), f32),
+            pltpu.SemaphoreType.DMA((3,)),
+            sem(2),
+            sem(count),
+            sem(2),
+            sem(2),
+            sem(around),
+        ],
+        compiler_params=pltpu.CompilerParams(
+            vmem_limit_bytes=40 * 2**20, collective_id=2, has_side_effects=True
+        ),
+    )(diffusivity, mixing, loss_matrix, previous, pair_matrix)
+
+
 def solution(mesh):
     placed = (P("lev", None, "lon"), P("lev", None, None), P("lev", None, None), P("lev"), P("lev"))
     return jax.shard_map(
-        local,
+        local_pairs if mesh.shape["lev"] == 4 else local,
         mesh=mesh,
         in_specs=placed,
         out_specs=(P("lev", None, "lon"), P("lev", None)),

time: 71.5 us -> 48.6 us (0.68)
  Pallas kernels: 68 us -> 41.6 us
  local copies, waits for them, and re-layouts: 2.97 us -> 6.11 us
    pallas_call x3 -> x1, Pallas kernels: 68 us -> 41.6 us  [local_pairs(): pl.pallas_call(step_kernel, out_shape=[jax.ShapeDtypeStruct((levels, size...]
    unnamed x4 -> x12, local copies, waits for them, and re-layouts: 2.97 us -> 6.11 us
where the time goes in v1:
time: 48.6 us; the launch traced here: 48.4 us
  Pallas kernels  41.6 us (86%)
  local copies, waits for them, and re-layouts  6.11 us (13%)
  between operations  0.65 us (1%)
    pallas_call x1, Pallas kernels, local_pairs(): pl.pallas_call(step_kernel, out_shape=[jax.ShapeDtypeStruct((levels, size...  41.6 us
    unnamed x12, local copies, waits for them, and re-layouts  6.11 us

profile of v1, /device:TPU:0, one launch (start us, length us, event | category | flops | bytes accessed | tf_op | source)
XLA Modules:
  0.0 48.4 jit_solution(9787819689125609269)
XLA Ops:
  0.6 0.0 copy-start
  0.6 1.3 %copy-done = f32[9,64,512]{2,1,0:T(8,128)S(1)} copy-done((f32[9,64,512]{2,1,0:T(8,128)S(1)}, f32[9,64,512]{2,1,0:T(8,128)}, u32[]{:S(2)}) %copy-start) | copy-done | bytes 1179672
  1.9 0.0 copy-start.1
  1.9 1.0 %copy-done.1 = f32[9,64,64]{2,1,0:T(8,128)S(1)} copy-done((f32[9,64,64]{2,1,0:T(8,128)S(1)}, f32[9,64,64]{2,1,0:T(8,128)}, u32[]{:S(2)}) %copy-start.1) | copy-done | bytes 147480
  2.9 0.0 copy-start.2
  2.9 1.0 %copy-done.2 = f32[9,64,64]{2,1,0:T(8,128)S(1)} copy-done((f32[9,64,64]{2,1,0:T(8,128)S(1)}, f32[9,64,64]{2,1,0:T(8,128)}, u32[]{:S(2)}) %copy-start.2) | copy-done | bytes 147480
  3.8 0.0 copy-start.3
  3.8 0.7 %copy-done.3 = f32[9]{0:T(128)S(1)} copy-done((f32[9]{0:T(128)S(1)}, f32[9]{0:T(128)}, u32[]{:S(2)}) %copy-start.3) | copy-done | bytes 60
  4.5 0.0 copy-start.4
  4.5 0.7 %copy-done.4 = f32[9]{0:T(128)S(1)} copy-done((f32[9]{0:T(128)S(1)}, f32[9]{0:T(128)}, u32[]{:S(2)}) %copy-start.4) | copy-done | bytes 60
  5.1 41.6 %shard_map.68 = (f32[9,64,512]{2,1,0:T(8,128)S(1)}, f32[9,64]{1,0:T(8,128)S(1)}) custom-call(f32[9]{0:T(128)S(1)} %copy-done.3, f32[9]{0:T(128)S(1)} %copy-done.4, f32[9,64,64]{2,1,0:T(8,128)S(1)} %copy-done.1, f32[9,64,512]{2,1,0:T(8,128)S(1)} %copy-done, f32[9,64,64]{2,1,0:T(8,128)S(1)} %copy-done.2), custom_call_target="tpu_custom_call" | custom-call | tf_op jit(solution)/shard_map/pallas_call | solution.py:980
  46.7 1.0 %copy.9 = f32[9,64,512]{2,1,0:T(8,128)} copy(f32[9,64,512]{2,1,0:T(8,128)S(1)} %get-tuple-element.4) | data formatting | bytes 2359296
  47.8 0.6 %copy.10 = f32[9,64]{1,0:T(8,128)} copy(f32[9,64]{1,0:T(8,128)S(1)} %get-tuple-element.5) | data formatting | bytes 4608
Async XLA Ops:
  0.6 1.3 %copy-start = (f32[9,64,512]{2,1,0:T(8,128)S(1)}, f32[9,64,512]{2,1,0:T(8,128)}, u32[]{:S(2)}) copy-start(f32[9,64,512]{2,1,0:T(8,128)} %prev_hbm.1) | copy-start | bytes 3538948
  1.9 1.0 %copy-start.1 = (f32[9,64,64]{2,1,0:T(8,128)S(1)}, f32[9,64,64]{2,1,0:T(8,128)}, u32[]{:S(2)}) copy-start(f32[9,64,64]{2,1,0:T(8,128)} %loss_hbm.1) | copy-start | bytes 442372
  2.9 1.0 %copy-start.2 = (f32[9,64,64]{2,1,0:T(8,128)S(1)}, f32[9,64,64]{2,1,0:T(8,128)}, u32[]{:S(2)}) copy-start(f32[9,64,64]{2,1,0:T(8,128)} %pair_hbm.1) | copy-start | bytes 442372
  3.8 0.7 %copy-start.3 = (f32[9]{0:T(128)S(1)}, f32[9]{0:T(128)}, u32[]{:S(2)}) copy-start(f32[9]{0:T(128)} %links_ref.1) | copy-start | bytes 112
  4.5 0.7 %copy-start.4 = (f32[9]{0:T(128)S(1)}, f32[9]{0:T(128)}, u32[]{:S(2)}) copy-start(f32[9]{0:T(128)} %mix_ref.1) | copy-start | bytes 112

commit v2 on v1

--- a/solution.py
+++ b/solution.py
@@ -562,6 +562,12 @@
     return jnp.dot(a, b, preferred_element_type=jnp.float32)
 
 
+def near_dot(a, b):
+    return lax.dot_general(
+        a, b, (((1,), (0,)), ((), ())), precision=lax.Precision.HIGH, preferred_element_type=jnp.float32
+    )
+
+
 def pull(links, loss):
     stiff = links[0]
     for a in links[1:]:
@@ -580,7 +586,7 @@
 
 def gains_for(ratio):
     rho, gains = (ratio - 1.0) / (ratio + 1.0), []
-    while rho > 1.5e-4:
+    while rho > 1.2e-3:
         gains.append(2.0 / (2.0 - rho * rho))
         rho = rho * rho / (2.0 - rho * rho)
     return gains
@@ -598,14 +604,16 @@
         rests.append(rest)
     rests = [gains[0] * dot(r, r) - (gains[0] - 1.0) * unit for r in rests]
     for step, g in enumerate(gains[1:]):
-        if step + 2 == len(gains):
-            xs = [g * (x + dot(x, r)) for x, r in zip(xs, rests)]
+        left = len(gains) - step - 2
+        mul = dot if left > 2 else near_dot
+        if left == 0:
+            xs = [g * (x + mul(x, r)) for x, r in zip(xs, rests)]
             break
-        both = [dot(jnp.concatenate([x, r], axis=0), r) for x, r in zip(xs, rests)]
+        both = [mul(jnp.concatenate([x, r], axis=0), r) for x, r in zip(xs, rests)]
         xs = [g * (x + b[:size]) for x, b in zip(xs, both)]
         rests = [g * b[size:] - (g - 1.0) * unit for b in both]
     rests = [unit - dot(a, x) for a, x in zip(blocks, xs)]
-    return [x + dot(x, r) for x, r in zip(xs, rests)]
+    return [x + near_dot(x, r) for x, r in zip(xs, rests)]
 
 
 def chain_factor(diag, links, floors, panel_ref, hook):
@@ -731,10 +739,10 @@
 
 
 def step_kernel(
-    links_ref, mix_ref, loss_hbm, prev_hbm, pair_hbm, out_ref, var_ref,
+    links_hbm, mix_hbm, loss_hbm, prev_hbm, pair_hbm, out_ref, var_ref, links_ref, mix_ref,
     loss_ref, prev_ref, pair_ref, pairs_ref, edges, halo, z_high, z_low, send_ref, all_ref,
     ends_high, ends_low, table_ref, sep_ref, f_high, f_low, part_ref, own_ref, near_ref, mine_ref, far_ref,
-    side_high, side_low, hq_high, hq_low, u_ref, top_ref, cur_ref, sums_ref, panel_ref,
+    side_high, side_low, hq_high, hq_low, u_ref, top_ref, cur_ref, sums_ref, panel_ref, w_ref, v_ref,
     load_sems, halo_sems, block_sems, near_sems, far_sems, sum_sems,
 ):
     levels, size, columns = prev_hbm.shape
@@ -750,15 +758,18 @@
         pltpu.make_async_copy(loss_hbm, loss_ref, load_sems.at[0]),
         pltpu.make_async_copy(prev_hbm, prev_ref.at[:, :, pl.ds(0, columns)], load_sems.at[1]),
         pltpu.make_async_copy(pair_hbm, pair_ref, load_sems.at[2]),
-    ]
-    for load in loads:
-        load.start()
+        pltpu.make_async_copy(links_hbm, links_ref, load_sems.at[3]),
+        pltpu.make_async_copy(mix_hbm, mix_ref, load_sems.at[4]),
+    ]
+    for k in (3, 0, 1, 2, 4):
+        loads[k].start()
     barrier = pltpu.get_barrier_semaphore()
     partners = [{"lev": lax.rem(me + d, count)} for d in range(1, count)]
     partners += [{"lon": lax.rem(place + d, around)} for d in range(1, around)]
     for device in partners:
         pl.semaphore_signal(barrier, inc=1, device_id=device, device_id_type=pl.DeviceIdType.MESH)
 
+    loads[3].wait()
     links = [jnp.full((1, 1), links_ref[k]) for k in range(levels)]
     on_diag = eye_of(size)
     halo_moves = halo_copies(edges, halo, halo_sems)
@@ -802,23 +813,27 @@
     all_ref[me] = send_ref[...]
 
     ends_high[...], ends_low[...] = split(jnp.concatenate([a * first, b * last], axis=1))
-    w_wide, (v_high, v_low) = wide(w), split(v)
-    v_wide = jnp.concatenate([v_high, v_high, v_low, jnp.zeros_like(v_high)], axis=1)
-    for k in range(0, inner, 2):
+    w_ref[...] = wide(w)
+    v_high, v_low = split(v)
+    v_ref[...] = jnp.concatenate([v_high, v_high, v_low, jnp.zeros_like(v_high)], axis=1)
+
+    def form(lo, hi):
+        spot = slice(lo * size, hi * size)
         new = lax.dot_general(
-            w_wide, v_wide[k * size : (k + 2) * size], (((1,), (1,)), ((), ())), preferred_element_type=jnp.float32
+            w_ref[spot], v_ref[...], (((1,), (1,)), ((), ())), preferred_element_type=jnp.float32
         )
-        for lo, hi in ((0, mid), (mid, mid + 1), (mid + 1, inner)):
-            piece = new[lo * size : hi * size]
-            if lo != mid and (lo <= k < hi or lo <= k + 1 < hi):
-                old = [
-                    panel_ref[j, lo * size : hi * size] if lo <= j < hi else jnp.zeros((piece.shape[0], size), jnp.float32)
-                    for j in (k, k + 1)
-                ]
-                piece = piece + jnp.concatenate(old, axis=1)
-            spot = slice(lo * size, hi * size), slice(k * size, (k + 2) * size)
-            z_high[spot], z_low[spot] = split(piece)
+        start, stop = (0, mid) if lo < mid else (mid + 1, inner)
+        if lo != mid:
+            zeros = jnp.zeros((new.shape[0], size), jnp.float32)
+            new = new + jnp.concatenate(
+                [panel_ref[j, spot] if start <= j < stop else zeros for j in range(inner)], axis=1
+            )
+        z_high[spot], z_low[spot] = split(new)
+
+    form(0, 1)
+    form(inner - 1, inner)
     loads[2].wait()
+    loads[4].wait()
     for k in range(levels):
         pairs_ref[k] = wide(pair_ref[k])
     for move in halo_moves:
@@ -847,8 +862,7 @@
         return copy
 
     def middle(width):
-        for k in range(1, inner - 1):
-            part_ref[k * size : (k + 1) * size, :width] = z_rows(k * size, (k + 1) * size, width)
+        part_ref[size:-size, :width] = z_rows(size, (inner - 1) * size, width)
 
     def merge(turn, width):
         upper = core == 0
@@ -862,17 +876,32 @@
 
     def condense(turn, width, tail, k_high, k_low):
         mine_ref[turn, :, :width] = tail + cat3(k_high, k_low, side_high[:, :width], side_low[:, :width])
-        copy = send(
-            mine_ref.at[turn, :, pl.ds(0, width)], far_ref.at[turn, :, pl.ds(0, width)], far_sems, turn,
-            {"lev": across},
-        )
-        start_all([copy])
-        return copy
+        half, quarter = columns // 2, columns // 4
+        first = pl.ds(pl.multiple_of(core * half, 128), quarter)
+        second = pl.ds(pl.multiple_of(core * half + quarter, 128), quarter)
+        routes = [(mine_ref, first, across), (mine_ref, second, across), (mine_ref, second, lax.rem(partner + 2, count))]
+        routes += [(mine_ref, pl.ds(columns, width - columns), across)] if width > columns else []
+        routes += [(far_ref, first, partner)]
+        copies = [
+            send(src.at[turn, :, spot], far_ref.at[turn, :, spot], far_sems, 5 * turn + k, {"lev": device})
+            for k, (src, spot, device) in enumerate(routes)
+        ]
+        start_all(copies[:-1])
+        return copies
+
+    def relay_far(copies):
+        copies[0].wait_recv()
+        start_all(copies[-1:])
+
+    def wait_far(copies):
+        copies[0].wait_send()
+        for copy in copies[1:]:
+            copy.wait()
 
     def gather_sides(width):
+        rest = cat3(hq_high[...], hq_low[...], side_high[:, :width], side_low[:, :width])
         for k in range(levels):
-            spot = slice(k * size, (k + 1) * size)
-            rows = cat3(hq_high[spot], hq_low[spot], side_high[:, :width], side_low[:, :width])
+            rows = rest[k * size : (k + 1) * size]
             cur_ref[k, :, :width] = rows if k == 0 else rows + part_ref[(k - 1) * size : k * size, :width]
 
     def finish(turn, width, to_ref):
@@ -883,7 +912,6 @@
 
     forcing(mix_ref, prev_ref, prev_ref, pairs_ref, full, sep_ref, f_high, f_low)
     near = ends(0, full)
-    middle(full)
     for copy in blocks:
         copy.wait()
 
@@ -937,18 +965,23 @@
     hq_high[:size], hq_low[:size] = split(own_q)
     u_ref[size:] = wide(cat3(ends_high[...], ends_low[...], p_high, p_low))
     u_ref[:size] = wide(own_p)
+    for lo, hi in ((1, mid), (mid, mid + 1), (mid + 1, inner - 1)):
+        form(lo, hi)
+    relay_far(far)
+    middle(full)
     gather_sides(full)
-    far.wait()
+    wait_far(far)
     finish(0, full, cur_ref)
 
     forcing(mix_ref, cur_ref, prev_ref, pairs_ref, columns, sep_ref, f_high, f_low)
     near = ends(1, columns)
-    middle(columns)
     near.wait()
     tail = merge(1, columns)
     far = condense(1, columns, tail, k_high, k_low)
+    middle(columns)
     gather_sides(columns)
-    far.wait()
+    relay_far(far)
+    wait_far(far)
     finish(1, columns, out_ref)
     lane = lax.broadcasted_iota(jnp.int32, (size, 128), 1)
     total = jnp.zeros((size, 128), jnp.float32)
@@ -983,9 +1016,11 @@
             jax.ShapeDtypeStruct((levels, size, columns), f32),
             jax.ShapeDtypeStruct((levels, size), f32),
         ],
-        in_specs=[SMEM, SMEM, hbm, hbm, hbm],
+        in_specs=[hbm] * 5,
         out_specs=[VMEM, VMEM],
         scratch_shapes=[
+            pltpu.SMEM((levels,), f32),
+            pltpu.SMEM((levels,), f32),
             buf((levels, size, size), f32),
             buf((levels, size, full), f32),
             buf((levels, size, size), f32),
@@ -1016,23 +1051,30 @@
             buf((levels, size, full), f32),
             buf((around, -(-levels // 8) * 8, size), f32),
             buf((levels - 1, inner, size), f32),
-            pltpu.SemaphoreType.DMA((3,)),
+            buf((inner, 4 * size), bf16),
+            buf((inner, 4 * size), bf16),
+            pltpu.SemaphoreType.DMA((5,)),
             sem(2),
             sem(count),
             sem(2),
-            sem(2),
+            sem(10),
             sem(around),
         ],
         compiler_params=pltpu.CompilerParams(
             vmem_limit_bytes=40 * 2**20, collective_id=2, has_side_effects=True
         ),
-    )(diffusivity, mixing, loss_matrix, previous, pair_matrix)
+    )(*(pltpu.with_memory_space_constraint(x, pltpu.MemorySpace.HBM) for x in (diffusivity, mixing, loss_matrix, previous, pair_matrix)))
+
+
+def chosen(previous, *rest):
+    paired = lax.axis_size("lev") == 4 and previous.shape[2] % 512 == 0
+    return (local_pairs if paired else local)(previous, *rest)
 
 
 def solution(mesh):
     placed = (P("lev", None, "lon"), P("lev", None, None), P("lev", None, None), P("lev"), P("lev"))
     return jax.shard_map(
-        local_pairs if mesh.shape["lev"] == 4 else local,
+        chosen,
         mesh=mesh,
         in_specs=placed,
         out_specs=(P("lev", None, "lon"), P("lev", None)),

time: 48.6 us -> 40.4 us (0.83)
  local copies, waits for them, and re-layouts: 6.11 us -> 1.61 us
  Pallas kernels: 41.6 us -> 37.9 us
    unnamed x12 -> x2, local copies, waits for them, and re-layouts: 6.11 us -> 1.61 us
    pallas_call x1, Pallas kernels: 41.6 us -> 37.9 us  [local_pairs(): pl.pallas_call(step_kernel, out_shape=[jax.ShapeDtypeStruct((levels, size...]
where the time goes in v2:
time: 40.4 us; the launch traced here: 40.2 us
  Pallas kernels  37.9 us (94%)
  local copies, waits for them, and re-layouts  1.61 us (4%)
  between operations  0.64 us (2%)
    pallas_call x1, Pallas kernels, local_pairs(): pl.pallas_call(step_kernel, out_shape=[jax.ShapeDtypeStruct((levels, size...  37.9 us
    unnamed x2, local copies, waits for them, and re-layouts  1.61 us

profile of v2, /device:TPU:0, one launch (start us, length us, event | category | flops | bytes accessed | tf_op | source)
XLA Modules:
  0.0 40.2 jit_solution(7172070010310370845)
XLA Ops:
  0.6 37.9 %shard_map.68 = (f32[9,64,512]{2,1,0:T(8,128)S(1)}, f32[9,64]{1,0:T(8,128)S(1)}) custom-call(f32[9]{0:T(128)} %links_hbm.1, f32[9]{0:T(128)} %mix_hbm.1, f32[9,64,64]{2,1,0:T(8,128)} %loss_hbm.1, f32[9,64,512]{2,1,0:T(8,128)} %prev_hbm.1, f32[9,64,64]{2,1,0:T(8,128)} %pair_hbm.1), custom_call_target="tpu_custom_call" | custom-call | tf_op jit(solution)/shard_map/pallas_call | solution.py:1013
  38.6 1.0 %copy.9 = f32[9,64,512]{2,1,0:T(8,128)} copy(f32[9,64,512]{2,1,0:T(8,128)S(1)} %get-tuple-element.4) | data formatting | bytes 2359296
  39.6 0.6 %copy.10 = f32[9,64]{1,0:T(8,128)} copy(f32[9,64]{1,0:T(8,128)S(1)} %get-tuple-element.5) | data formatting | bytes 4608

commit v3 on v2

--- a/solution.py
+++ b/solution.py
@@ -619,7 +619,7 @@
 def chain_factor(diag, links, floors, panel_ref, hook):
     count, size = len(diag), diag[0].shape[0]
     unit = jnp.where(eye_of(size), 1.0, 0.0).astype(jnp.float32)
-    by_depth, thin = {}, {}
+    by_depth, thin, corners = {}, {}, {}
     plan(0, count, by_depth)
 
     def rows(lo, hi):
@@ -634,7 +634,7 @@
             t, thin_parts = floors[mid], []
             if lo < mid:
                 arm = links[mid] * panel_ref[mid - 1, rows(lo, mid)]
-                s = s - links[mid] * arm[-size:]
+                s = s - (links[mid] * links[mid]) * corners[lo, mid][1]
                 parts.append(arm)
                 thin_parts += [links[mid] * x for x in thin[lo, mid][-1]]
                 t = t - links[mid] * thin_parts[-1]
@@ -642,7 +642,7 @@
             thin_parts.append(1.0)
             if mid + 1 < hi:
                 arm = links[mid + 1] * panel_ref[mid + 1, rows(mid + 1, hi)]
-                s = s - links[mid + 1] * arm[:size]
+                s = s - (links[mid + 1] * links[mid + 1]) * corners[mid + 1, hi][0]
                 parts.append(arm)
                 thin_arm = [links[mid + 1] * x for x in thin[mid + 1, hi][0]]
                 t = t - links[mid + 1] * thin_arm[0]
@@ -660,7 +660,18 @@
                         thin[lo, hi][i - lo][j - lo] += thin[a, b][i - a][j - a]
             if hi - lo == 1:
                 panel_ref[mid, rows(mid, hi)] = z
+                corners[lo, hi] = z, z
                 continue
+            ends = v[:size], v[-size:]
+            arms_out = [dot(x, z) for x in ends]
+            corners[lo, hi] = tuple(
+                z if at == mid else corners[part][side] + dot_t(y, x)
+                for side, (at, part, x, y) in enumerate(
+                    ((lo, (lo, mid), ends[0], arms_out[0]), (hi - 1, (mid + 1, hi), ends[1], arms_out[1]))
+                )
+            )
+            if hi - lo == count:
+                far = dot_t(arms_out[1], ends[0])
             w = dot(v, z)
             if hi - lo == count:
                 continue
@@ -677,7 +688,7 @@
                     panel_ref[k, rows(a, b)] = piece
         if depth < max(by_depth):
             hook(depth)
-    return v, w, by_depth[max(by_depth)][0][1], thin[0, count]
+    return v, w, by_depth[max(by_depth)][0][1], thin[0, count], (*corners[0, count], far)
 
 
 def fold(x):
@@ -788,20 +799,12 @@
         for k in range(levels)
     ]
     floors = [LEAST + links[k] + (links[k - 1] if k else 0.0) for k in range(levels)]
-    v, w, mid, thin = chain_factor(diag[1:], links[:inner], floors[1:], panel_ref, hook)
+    v, w, mid, thin, (z_first, z_last, z_far) = chain_factor(diag[1:], links[:inner], floors[1:], panel_ref, hook)
     a, b = links[0], links[inner]
-    old = [
-        panel_ref[0, : mid * size],
-        jnp.zeros((size, size), jnp.float32),
-        panel_ref[inner - 1, (mid + 1) * size :],
-    ]
-    tips = dot_t(w, jnp.concatenate([v[:size], v[-size:]], axis=0))
-    first = tips[:, :size] + jnp.concatenate([old[0], old[1], jnp.zeros_like(old[2])], axis=0)
-    last = tips[:, size:] + jnp.concatenate([jnp.zeros_like(old[0]), old[1], old[2]], axis=0)
     sub = lax.broadcasted_iota(jnp.int32, (8, 128), 0)
-    send_ref[: size // 2] = fold(diag[0] - a * a * first[:size])
-    send_ref[size // 2 : size] = fold(jnp.where(on_diag, b, 0.0) - b * b * last[-size:])
-    send_ref[size : 3 * size // 2] = fold(a * b * first[-size:])
+    send_ref[: size // 2] = fold(diag[0] - a * a * z_first)
+    send_ref[size // 2 : size] = fold(jnp.where(on_diag, b, 0.0) - b * b * z_last)
+    send_ref[size : 3 * size // 2] = fold(a * b * z_far)
     send_ref[3 * size // 2 :] = jnp.where(
         sub == 0, floors[0] - a * a * thin[0][0], jnp.where(sub == 1, b - b * b * thin[-1][-1], a * b * thin[0][-1])
     )
@@ -812,6 +815,14 @@
     start_all(blocks)
     all_ref[me] = send_ref[...]
 
+    old = [
+        panel_ref[0, : mid * size],
+        jnp.zeros((size, size), jnp.float32),
+        panel_ref[inner - 1, (mid + 1) * size :],
+    ]
+    tips = dot_t(w, jnp.concatenate([v[:size], v[-size:]], axis=0))
+    first = tips[:, :size] + jnp.concatenate([old[0], old[1], jnp.zeros_like(old[2])], axis=0)
+    last = tips[:, size:] + jnp.concatenate([jnp.zeros_like(old[0]), old[1], old[2]], axis=0)
     ends_high[...], ends_low[...] = split(jnp.concatenate([a * first, b * last], axis=1))
     w_ref[...] = wide(w)
     v_high, v_low = split(v)
@@ -912,6 +923,9 @@
 
     forcing(mix_ref, prev_ref, prev_ref, pairs_ref, full, sep_ref, f_high, f_low)
     near = ends(0, full)
+    for lo, hi in ((1, mid), (mid, mid + 1), (mid + 1, inner - 1)):
+        form(lo, hi)
+    middle(full)
     for copy in blocks:
         copy.wait()
 
@@ -965,10 +979,7 @@
     hq_high[:size], hq_low[:size] = split(own_q)
     u_ref[size:] = wide(cat3(ends_high[...], ends_low[...], p_high, p_low))
     u_ref[:size] = wide(own_p)
-    for lo, hi in ((1, mid), (mid, mid + 1), (mid + 1, inner - 1)):
-        form(lo, hi)
     relay_far(far)
-    middle(full)
     gather_sides(full)
     wait_far(far)
     finish(0, full, cur_ref)
@@ -988,7 +999,9 @@
     for k in range(levels):
         row = out_ref[k]
         total = jnp.where(lane == k, jnp.sum(row * row, axis=1, keepdims=True), total)
-    sums_ref[0] = total.T[: sums_ref.shape[1]]
+    held = sums_ref.shape[1]
+    total = total.T
+    sums_ref[0] = jnp.concatenate([total[:held], total[held : 2 * held]], axis=1)
     copies = [
         send(sums_ref.at[0], sums_ref.at[d], sum_sems, d, {"lon": lax.rem(place + d, around)})
         for d in range(1, around)
@@ -999,7 +1012,20 @@
     total = sums_ref[place]
     for j in range(1, around):
         total = total + sums_ref[lax.rem(place - j + around, around)]
-    var_ref[...] = (total / (columns * around))[:levels]
+    total = total / (columns * around)
+    total = jnp.concatenate([total[:, :size], total[:, size:]], axis=0)
+    var_ref[...] = total[:levels]
+
+
+def hand_out(from_out, from_var, to_out, to_var, sems):
+    copies = [
+        pltpu.make_async_copy(from_out, to_out, sems.at[0]),
+        pltpu.make_async_copy(from_var, to_var, sems.at[1]),
+    ]
+    for copy in copies:
+        copy.start()
+    for copy in copies:
+        copy.wait()
 
 
 def local_pairs(previous, loss_matrix, pair_matrix, diffusivity, mixing):
@@ -1010,7 +1036,7 @@
     buf, sem = pltpu.VMEM, lambda n: pltpu.SemaphoreType.DMA((2, n))
     hbm = pl.BlockSpec(memory_space=pltpu.MemorySpace.HBM)
     packed = 3 * size // 2 + 8
-    return pl.pallas_call(
+    results = pl.pallas_call(
         step_kernel,
         out_shape=[
             jax.ShapeDtypeStruct((levels, size, columns), f32),
@@ -1049,7 +1075,7 @@
             buf((levels * size, 4 * size), bf16),
             buf((size, 4 * size), bf16),
             buf((levels, size, full), f32),
-            buf((around, -(-levels // 8) * 8, size), f32),
+            buf((around, -(-levels // 16) * 8, 2 * size), f32),
             buf((levels - 1, inner, size), f32),
             buf((inner, 4 * size), bf16),
             buf((inner, 4 * size), bf16),
@@ -1064,6 +1090,14 @@
             vmem_limit_bytes=40 * 2**20, collective_id=2, has_side_effects=True
         ),
     )(*(pltpu.with_memory_space_constraint(x, pltpu.MemorySpace.HBM) for x in (diffusivity, mixing, loss_matrix, previous, pair_matrix)))
+    return pl.pallas_call(
+        hand_out,
+        out_shape=[jax.ShapeDtypeStruct(x.shape, x.dtype) for x in results],
+        in_specs=[VMEM, VMEM],
+        out_specs=[hbm, hbm],
+        scratch_shapes=[pltpu.SemaphoreType.DMA((2,))],
+        compiler_params=pltpu.CompilerParams(vmem_limit_bytes=2**20),
+    )(*results)
 
 
 def chosen(previous, *rest):

time: 40.4 us -> 38.8 us (0.960)
  local copies, waits for them, and re-layouts: 1.61 us -> 0 us
    unnamed x2 -> x0, local copies, waits for them, and re-layouts: 1.61 us -> none
    pallas_call x0 -> x1, Pallas kernels: none -> 1.03 us  [local_pairs(): pl.pallas_call(hand_out, out_shape=[jax.ShapeDtypeStruct(x.shape, x.dtype...]
    pallas_call x1, Pallas kernels: 37.9 us -> 37 us  [local_pairs(): pl.pallas_call(step_kernel, out_shape=[jax.ShapeDtypeStruct((levels, size...]
where the time goes in v3:
time: 38.8 us; the launch traced here: 38.7 us
  Pallas kernels  38 us (98%)
  between operations  0.64 us (2%)
    pallas_call x1, Pallas kernels, local_pairs(): pl.pallas_call(step_kernel, out_shape=[jax.ShapeDtypeStruct((levels, size...  37 us
    pallas_call x1, Pallas kernels, local_pairs(): pl.pallas_call(hand_out, out_shape=[jax.ShapeDtypeStruct(x.shape, x.dtype...  1.03 us

profile of v3, /device:TPU:0, one launch (start us, length us, event | category | flops | bytes accessed | tf_op | source)
XLA Modules:
  0.0 38.7 jit_solution(8693955477907543138)
XLA Ops:
  0.6 37.0 %shard_map.68 = (f32[9,64,512]{2,1,0:T(8,128)S(1)}, f32[9,64]{1,0:T(8,128)S(1)}) custom-call(f32[9]{0:T(128)} %links_hbm.1, f32[9]{0:T(128)} %mix_hbm.1, f32[9,64,64]{2,1,0:T(8,128)} %loss_hbm.1, f32[9,64,512]{2,1,0:T(8,128)} %prev_hbm.1, f32[9,64,64]{2,1,0:T(8,128)} %pair_hbm.1), custom_call_target="tpu_custom_call" | custom-call | tf_op jit(solution)/shard_map/pallas_call | solution.py:1039
  37.6 1.0 %shard_map.69 = (f32[9,64,512]{2,1,0:T(8,128)}, f32[9,64]{1,0:T(8,128)}) custom-call(f32[9,64,512]{2,1,0:T(8,128)S(1)} %get-tuple-element.4.from_out, f32[9,64]{1,0:T(8,128)S(1)} %get-tuple-element.5.from_var), custom_call_target="tpu_custom_call" | custom-call | tf_op jit(solution)/shard_map/pallas_call | solution.py:1093

commit v4 on v3

--- a/solution.py
+++ b/solution.py
@@ -582,6 +582,17 @@
         draws = itertools.product((200.0, 2000.0), repeat=min(count, 8) + 1)
         sides.append([(pull(d, 640.0), pull(d, 0.05)) for d in draws])
     return 1.15 * max((641.0 + a + c) / (1.05 + b + d) for a, b in sides[0] for c, d in sides[1])
+
+
+def edge_ratios(inner):
+    inner = min(inner, 8)
+    held = [(pull(d, 640.0), pull(d, 0.05)) for d in itertools.product((200.0, 2000.0), repeat=inner + 1)]
+    draws = [(0.0, *d) for d in itertools.product((200.0, 2000.0), repeat=inner + 1)]
+    free = [(pull(d, 640.0), pull(d, 0.05)) for d in draws]
+    outer = max((641.0 + a) / (1.05 + b) for a, b in held)
+    outer = max(outer, max((320.5 + a) / (0.525 + b) for a, b in held))
+    second = max((641.0 + a + c) / (1.05 + b + d) for a, b in held for c, d in free)
+    return 1.15 * outer, 1.15 * second
 
 
 def gains_for(ratio):
@@ -941,11 +952,12 @@
     t = [floor(k, 0) + (floor(k - 1, 1) if k else 0.0) for k in range(count)]
     c = [None] + [block(k, 2) for k in range(count - 1)]
     e = [None] + [floor(k, 2) for k in range(count - 1)]
-    z0, z3 = invert_fixed([s[0], s[3]], [0.97 * t[0], 0.97 * t[3]], ratio)
+    outer, second = edge_ratios(inner)
+    z0, z3 = invert_fixed([s[0], s[3]], [0.97 * t[0], 0.97 * t[3]], outer)
     a1, a3 = dot(c[1], z0), dot(z3, c[3])
     s1 = s[1] - dot_t(a1, c[1])
     t1 = t[1] - e[1] * e[1] / t[0]
-    (z1,) = invert_fixed([s1], [0.97 * t1], ratio)
+    (z1,) = invert_fixed([s1], [0.97 * t1], second)
     a2 = dot(c[2], z1)
     s2 = s[2] - dot_t(a2, c[2]) - dot(c[3], a3, ((0,), (0,)))
     t2 = t[2] - e[2] * e[2] / t1 - e[3] * e[3] / t[3]

time: 38.8 us -> 38 us (0.979)
  Pallas kernels: 38 us -> 37.2 us
    pallas_call x1, Pallas kernels: 37 us -> 36.1 us  [local_pairs(): pl.pallas_call(step_kernel, out_shape=[jax.ShapeDtypeStruct((levels, size...]
where the time goes in v4:
time: 38 us; the launch traced here: 37.8 us
  Pallas kernels  37.2 us (98%)
  between operations  0.64 us (2%)
    pallas_call x1, Pallas kernels, local_pairs(): pl.pallas_call(step_kernel, out_shape=[jax.ShapeDtypeStruct((levels, size...  36.1 us
    pallas_call x1, Pallas kernels, local_pairs(): pl.pallas_call(hand_out, out_shape=[jax.ShapeDtypeStruct(x.shape, x.dtype...  1.03 us

profile of v4, /device:TPU:0, one launch (start us, length us, event | category | flops | bytes accessed | tf_op | source)
XLA Modules:
  0.0 37.8 jit_solution(3212019341436589004)
XLA Ops:
  0.6 36.1 %shard_map.68 = (f32[9,64,512]{2,1,0:T(8,128)S(1)}, f32[9,64]{1,0:T(8,128)S(1)}) custom-call(f32[9]{0:T(128)} %links_hbm.1, f32[9]{0:T(128)} %mix_hbm.1, f32[9,64,64]{2,1,0:T(8,128)} %loss_hbm.1, f32[9,64,512]{2,1,0:T(8,128)} %prev_hbm.1, f32[9,64,64]{2,1,0:T(8,128)} %pair_hbm.1), custom_call_target="tpu_custom_call" | custom-call | tf_op jit(solution)/shard_map/pallas_call | solution.py:1051
  36.8 1.0 %shard_map.69 = (f32[9,64,512]{2,1,0:T(8,128)}, f32[9,64]{1,0:T(8,128)}) custom-call(f32[9,64,512]{2,1,0:T(8,128)S(1)} %get-tuple-element.4.from_out, f32[9,64]{1,0:T(8,128)S(1)} %get-tuple-element.5.from_var), custom_call_target="tpu_custom_call" | custom-call | tf_op jit(solution)/shard_map/pallas_call | solution.py:1105

commit v5 on v4

--- a/solution.py
+++ b/solution.py
@@ -683,7 +683,7 @@
             )
             if hi - lo == count:
                 far = dot_t(arms_out[1], ends[0])
-            w = dot(v, z)
+            w = near_dot(v, z) if hi - lo == count else dot(v, z)
             if hi - lo == count:
                 continue
             new = dot_t(w, v)
@@ -961,8 +961,8 @@
     a2 = dot(c[2], z1)
     s2 = s[2] - dot_t(a2, c[2]) - dot(c[3], a3, ((0,), (0,)))
     t2 = t[2] - e[2] * e[2] / t1 - e[3] * e[3] / t[3]
-    b1 = dot(z1, a1)
-    p0 = dot(a2, a1)
+    b1 = near_dot(z1, a1)
+    p0 = near_dot(a2, a1)
     zero = jnp.zeros((size, size), jnp.float32)
     unit = jnp.where(on_diag, 1.0, 0.0).astype(jnp.float32)
     sides = [

time: 38 us -> 38 us (level)
  no operation moved by 1% of the time
where the time goes in v5:
time: 38 us; the launch traced here: 37.8 us
  Pallas kernels  37.2 us (98%)
  between operations  0.64 us (2%)
    pallas_call x1, Pallas kernels, local_pairs(): pl.pallas_call(step_kernel, out_shape=[jax.ShapeDtypeStruct((levels, size...  36.2 us
    pallas_call x1, Pallas kernels, local_pairs(): pl.pallas_call(hand_out, out_shape=[jax.ShapeDtypeStruct(x.shape, x.dtype...  1.03 us

profile of v5, /device:TPU:0, one launch (start us, length us, event | category | flops | bytes accessed | tf_op | source)
XLA Modules:
  0.0 37.8 jit_solution(3967433217027586564)
XLA Ops:
  0.6 36.2 %shard_map.68 = (f32[9,64,512]{2,1,0:T(8,128)S(1)}, f32[9,64]{1,0:T(8,128)S(1)}) custom-call(f32[9]{0:T(128)} %links_hbm.1, f32[9]{0:T(128)} %mix_hbm.1, f32[9,64,64]{2,1,0:T(8,128)} %loss_hbm.1, f32[9,64,512]{2,1,0:T(8,128)} %prev_hbm.1, f32[9,64,64]{2,1,0:T(8,128)} %pair_hbm.1), custom_call_target="tpu_custom_call" | custom-call | tf_op jit(solution)/shard_map/pallas_call | solution.py:1051
  36.8 1.0 %shard_map.69 = (f32[9,64,512]{2,1,0:T(8,128)}, f32[9,64]{1,0:T(8,128)}) custom-call(f32[9,64,512]{2,1,0:T(8,128)S(1)} %get-tuple-element.4.from_out, f32[9,64]{1,0:T(8,128)S(1)} %get-tuple-element.5.from_var), custom_call_target="tpu_custom_call" | custom-call | tf_op jit(solution)/shard_map/pallas_call | solution.py:1105
